TPU v7x, 32 devices: a whole 2x2x4 slice. The times are simulated.
32 devices in a mesh: gx: 2 (over x), gy: 4 (over z), gz: 4 (over y, core).
Axes of the slice: x: 2, y: 2, z: 4, core: 2. Of those that a mesh axis runs over, the one named last changes fastest.
Arguments:
- right_side: float32 [16, 64, 512], P('gx', 'gy', 'gz'), may hold values from -40 to 40
- fiber_class: int32 [16, 64, 512], P('gx', 'gy', 'gz'), may hold values from 0 to 15
- conductivity_scale: float32 [16, 64, 512], P('gx', 'gy', 'gz'), may hold values from 0.8 to 1.25
- class_tensor: float32 [6, 16], replicated, may hold values from -0.15 to 1.8, as said below
- block_ids: int32 [2, 4, 8], replicated, may hold values from 0 to 63, as said below
Outputs:
- solution: float32 [16, 64, 512], P('gx', 'gy', 'gz')
- residual: float32 [16, 64, 512], P('gx', 'gy', 'gz')
Inputs may be any that keep to these rules, and one draw needn't show every extreme that they name: `class_tensor`: column k is the tensor t I + (l - t) f f^T for a unit vector f, with 1 <= t <= 1.5 and 1.05 <= l / t <= 1.2. `block_ids`: each subdomain number names exactly 1 block.
All inputs are finite; a program needn't handle non-finite values.
Results may differ from a plain program's by a relative error of at most 0.0003.
Values sent between devices are 32-bit elements; how exact they have to be, the bound alone decides.
A program may use at most 64 MiB of HBM per device.

v0:
```python
import jax
import jax.numpy as jnp
from jax import lax
from jax.sharding import PartitionSpec as P

CX = 8
CY = 16
CZ = 128
ZBLK = 2
BZ = 64
COARSE = 64
NCLS = 16
ITERS = 2
STENCIL_TAPS = (
    (1, 0, 0, 0, 1.0),
    (-1, 0, 0, 0, 1.0),
    (0, 1, 0, 1, 1.0),
    (0, -1, 0, 1, 1.0),
    (0, 0, 1, 2, 1.0),
    (0, 0, -1, 2, 1.0),
    (1, 1, 0, 3, 0.5),
    (-1, -1, 0, 3, 0.5),
    (1, -1, 0, 3, -0.5),
    (-1, 1, 0, 3, -0.5),
    (1, 0, 1, 4, 0.5),
    (-1, 0, -1, 4, 0.5),
    (1, 0, -1, 4, -0.5),
    (-1, 0, 1, 4, -0.5),
    (0, 1, 1, 5, 0.5),
    (0, -1, -1, 5, 0.5),
    (0, 1, -1, 5, -0.5),
    (0, -1, 1, 5, -0.5),
)


def padded_2(cells, sides, width):
    for axis, dim in sides:
        count = lax.axis_size(axis)
        ends = count - 1
        head = lax.slice_in_dim(cells, 0, width, axis=dim)
        tail = lax.slice_in_dim(cells, cells.shape[dim] - width, cells.shape[dim], axis=dim)
        cells = jnp.concatenate(
            [
                lax.ppermute(tail, axis, [(i, (i + 1) % count) for i in range(ends)]),
                cells,
                lax.ppermute(head, axis, [((i + 1) % count, i) for i in range(ends)]),
            ],
            axis=dim,
        )
    return cells


def shifted(padded, step_x, step_y, step_z):
    width_x = padded.shape[-3] - 2
    width_y = padded.shape[-2] - 2
    width_z = padded.shape[-1] - 2
    return padded[
        1 + step_x : 1 + step_x + width_x,
        1 + step_y : 1 + step_y + width_y,
        1 + step_z : 1 + step_z + width_z,
    ]


def edge_weights(tensors, step_x, step_y, step_z, component, factor):
    layer = tensors[component]
    return 0.5 * factor * (shifted(layer, 0, 0, 0) + shifted(layer, step_x, step_y, step_z))


def operate(padded, tensors):
    centre = shifted(padded, 0, 0, 0)
    accumulated = jnp.zeros_like(centre)
    for step_x, step_y, step_z, component, factor in STENCIL_TAPS:
        weight = edge_weights(tensors, step_x, step_y, step_z, component, factor)
        accumulated = accumulated + weight * (centre - shifted(padded, step_x, step_y, step_z))
    return accumulated


def class_onehot(labels, count):
    return (labels[..., None] == jnp.arange(count, dtype=jnp.int32)).astype(jnp.float32)


def reach_onehot(length, offset):
    position = jnp.arange(length, dtype=jnp.int32)
    relative = (position + offset) // length + 1
    return (relative[:, None] == jnp.arange(3, dtype=jnp.int32)[None, :]).astype(jnp.float32)


def reach_blocks(length, offset, blocks):
    block_span = length // blocks
    position = jnp.arange(length, dtype=jnp.int32)
    owning = (position // block_span)[:, None] == jnp.arange(blocks, dtype=jnp.int32)[None, :]
    relative = ((position % block_span + offset) // block_span + 1)[:, None] == jnp.arange(
        3, dtype=jnp.int32
    )[None, :]
    return (owning[:, :, None] & relative[:, None, :]).astype(jnp.float32)


def centre_mask():
    places = jnp.arange(3, dtype=jnp.int32)
    return (
        (places[:, None, None] == 1) & (places[None, :, None] == 1) & (places[None, None, :] == 1)
    )


def build_tensors(matches, scale, class_tensor):
    return (
        jnp.stack(
            [
                jnp.sum(
                    jnp.where(matches, class_tensor[component][:, None, None, None], 0.0), axis=0
                )
                for component in range(6)
            ]
        )
        * scale[None]
    )


def body(right_side, fiber_class, conductivity_scale, class_tensor, block_ids):
    highest = lax.Precision.HIGHEST
    kinds = jnp.arange(NCLS, dtype=jnp.int32)
    matches = fiber_class[None] == kinds[:, None, None, None]
    local_tensor = build_tensors(matches, conductivity_scale, class_tensor)
    tensors = padded_2(local_tensor, (("gx", 1), ("gy", 2), ("gz", 3)), 1)
    place_x = lax.axis_index("gx")
    place_y = lax.axis_index("gy")
    place_z = lax.axis_index("gz")
    padded_ids = jnp.pad(block_ids, 1, constant_values=-1)
    window = lax.dynamic_slice(padded_ids, (place_x, place_y, place_z * ZBLK), (3, 3, ZBLK + 2))
    own_hot = class_onehot(window[1, 1, 1 : ZBLK + 1], COARSE)
    neighbours = jnp.stack([window[:, :, z_block : z_block + 3] for z_block in range(ZBLK)])
    rim_weight = jnp.zeros((ZBLK, 3, 3, 3), jnp.float32)
    for step_x, step_y, step_z, component, factor in STENCIL_TAPS:
        weight = edge_weights(tensors, step_x, step_y, step_z, component, factor)
        rim_weight = rim_weight + jnp.einsum(
            "xyz,xa,yb,zjc->jabc",
            weight,
            reach_onehot(CX, step_x),
            reach_onehot(CY, step_y),
            reach_blocks(CZ, step_z, ZBLK),
            precision=highest,
        )
    rim_weight = jnp.where(centre_mask()[None], 0.0, rim_weight)
    diagonal_terms = jnp.einsum(
        "jk,j->k", own_hot, jnp.sum(rim_weight, axis=(1, 2, 3)), precision=highest
    )
    coupling = jnp.einsum(
        "jk,jabc,jabcl->kl",
        own_hot,
        rim_weight,
        class_onehot(neighbours, COARSE),
        precision=highest,
    )
    coarse = lax.psum(jnp.diag(diagonal_terms) - coupling, ("gx", "gy", "gz"))
    coarse = 0.5 * (coarse + coarse.T)
    factor_lower = jnp.linalg.cholesky(coarse)

    def restrict(field):
        block_totals = jnp.sum(field.reshape(CX, CY, ZBLK, BZ), axis=(0, 1, 3))
        return jnp.einsum("jk,j->k", own_hot, block_totals, precision=highest)

    def prolong(coarse_values):
        values = jnp.einsum("jk,k->j", own_hot, coarse_values, precision=highest)
        return jnp.broadcast_to(values[None, None, :, None], (CX, CY, ZBLK, BZ)).reshape(CX, CY, CZ)

    def apply_field(field):
        padded = padded_2(field, (("gx", 0), ("gy", 1), ("gz", 2)), 1)
        return operate(padded, tensors)

    def coarse_solve(field):
        projected = lax.psum(restrict(field), ("gx", "gy", "gz"))
        return jax.scipy.linalg.cho_solve((factor_lower, True), projected)

    def deflation_image(coarse_values):
        result = apply_field(prolong(coarse_values))
        return result

    coarse_values = coarse_solve(right_side)
    coarse_part = prolong(coarse_values)
    residual = right_side - deflation_image(coarse_values)
    estimate = jnp.zeros_like(right_side)

    def joint_terms(field):
        product = apply_field(field)
        projected, norm_value, cross_value = lax.psum(
            (restrict(product), jnp.sum(field * field), jnp.sum(field * product)),
            ("gx", "gy", "gz"),
        )
        correction = jax.scipy.linalg.cho_solve((factor_lower, True), projected)
        image_field = product - deflation_image(correction)
        return (image_field, norm_value, cross_value - jnp.sum(projected * correction))

    image_field, norm_now, curvature_now = joint_terms(residual)
    step_size = norm_now / curvature_now
    direction = residual
    along = image_field
    for iteration in range(ITERS):
        estimate = estimate + step_size * direction
        residual = residual - step_size * along
        if iteration + 1 < ITERS:
            image_field, norm_next, curvature_now = joint_terms(residual)
            step_ratio = norm_next / norm_now
            step_size = norm_next / (curvature_now - step_ratio * norm_next / step_size)
            direction = residual + step_ratio * direction
            along = image_field + step_ratio * along
            norm_now = norm_next
    solution = coarse_part + estimate - prolong(coarse_solve(apply_field(estimate)))
    return (solution, residual)


def solution(mesh):
    placed = (P("gx", "gy", "gz"), P("gx", "gy", "gz"), P("gx", "gy", "gz"), P(), P())
    return jax.shard_map(
        body,
        mesh=mesh,
        in_specs=placed,
        out_specs=(P("gx", "gy", "gz"), P("gx", "gy", "gz")),
        check_vma=False,
    )
```

profile of v0, /device:TPU:0, one launch (start us, length us, event | category | flops | bytes accessed | tf_op | source)
XLA Modules:
  0.0 365.0 jit_solution(11324183408643841926)
XLA Ops:
  0.6 0.9 slice_bitcast_fusion.11
  1.6 1.7 select_reduce_fusion
  4.2 4.9 %collective-permute-start = (f32[6,1,16,128]{3,2,1,0:T(8,128)S(1)}, f32[6,1,16,128]{3,2,1,0:T(8,128)S(1)}, u32[]{:S(2)}, u32[]{:S(2)}) collective-permute-start(f32[6,1,16,128]{3,2,1,0:T(8,128)S(1)} %get-tuple-element.39), channel_id=1, source_target_pairs={{0,16},{1,17},{2,18},{3,19},{4,20},{5,21},{6,22},{7,23},{8,24},{9,... | collective-permute-start | bytes 147464 | tf_op jit(solution)/shard_map/ppermute | solution.py:44
  9.1 1.3 collective-permute-start.1
  11.4 3.7 %collective-permute-done.1 = f32[6,1,16,128]{3,2,1,0:T(8,128)S(1)} collective-permute-done((f32[6,1,16,128]{3,2,1,0:T(8,128)S(1)}, f32[6,1,16,128]{3,2,1,0:T(8,128)S(1)}, u32[]{:S(2)}, u32[]{:S(2)}) %collective-permute-start.1) | collective-permute-done | bytes 49184 | tf_op jit(solution)/shard_map/ppermute | solution.py:46
  15.1 3.5 collective-permute-start.2
  18.6 1.3 collective-permute-start.3
  20.2 4.2 %collective-permute-done.3 = f32[6,10,1,128]{3,2,1,0:T(1,128)S(1)} collective-permute-done((f32[6,10,1,128]{3,2,1,0:T(1,128)S(1)}, f32[6,10,1,128]{3,2,1,0:T(1,128)S(1)}, u32[]{:S(2)}, u32[]{:S(2)}) %collective-permute-start.3) | collective-permute-done | bytes 30752 | tf_op jit(solution)/shard_map/ppermute | solution.py:46
  25.2 1.3 collective-permute-start.4
  27.0 1.3 collective-permute-start.5
  28.8 3.0 collective-permute-done.5
  43.4 40.4 %all-reduce.3 = (f32[64,64]{1,0:T(8,128)S(1)}, f32[64]{0:T(128)S(1)}) all-reduce(f32[64,64]{1,0:T(8,128)S(1)} %convolution_subtract_fusion, f32[64]{0:T(128)S(1)} %convolution_bitcast_fusion.26), channel_id=1, replica_groups=mesh['gx'=2,'gy'=4,'gz'=4] {'gx','gy','gz'}, use_global_device_ids=true, to_apply=%region_7.8 | all-reduce | flops 4160 | bytes 33280 | tf_op jit(solution)/shard_map/psum | solution.py:154
  84.0 5.8 %cholesky.19 = f32[64,64]{1,0:T(8,128)S(1)} custom-call(f32[64,64]{1,0:T(8,128)S(1)} %fusion.262), custom_call_target="Cholesky" | custom-call | tf_op jit(solution)/shard_map/jit(cholesky)/cholesky | solution.py:156
  91.2 4.9 %custom-call.11 = f32[1,64,64]{1,2,0:T(8,128)S(1)} custom-call(f32[1,64,64]{2,1,0:T(8,128)S(1)} %fusion.251), custom_call_target="InvertDiagBlocksLowerTriangular" | custom-call | tf_op jit(solution)/shard_map/jit(_cho_solve)/triangular_solve | solution.py:172
  96.8 1.3 collective-permute-start.6
  98.1 4.5 %collective-permute-start.7 = (f32[1,16,128]{2,1,0:T(8,128)S(1)}, f32[1,16,128]{2,1,0:T(8,128)S(1)}, u32[]{:S(2)}, u32[]{:S(2)}) collective-permute-start(f32[1,16,128]{2,1,0:T(8,128)S(1)} %slice.1082), channel_id=1, source_target_pairs={{0,16},{1,17},{2,18},{3,19},{4,20},{5,21},{6,22},{7,23},{8,24},{9,... | collective-permute-start | bytes 24584 | tf_op jit(solution)/shard_map/ppermute | solution.py:44
  102.6 1.3 collective-permute-done.7
  104.0 1.3 collective-permute-start.8
  105.3 4.5 %collective-permute-start.9 = (f32[10,1,128]{2,1,0:T(1,128)S(1)}, f32[10,1,128]{2,1,0:T(1,128)S(1)}, u32[]{:S(2)}, u32[]{:S(2)}) collective-permute-start(f32[10,1,128]{2,1,0:T(1,128)S(1)} %get-tuple-element.105), channel_id=1, source_target_pairs={{0,4},{4,8},{8,12},{1,5},{5,9},{9,13},{2,6},{6,10},{10,14},{3,7},{... | collective-permute-start | bytes 15368 | tf_op jit(solution)/shard_map/ppermute | solution.py:44
  109.9 1.3 collective-permute-done.9
  111.3 1.3 collective-permute-start.10
  112.6 3.0 collective-permute-start.11
  115.7 0.9 collective-permute-done.11
  117.0 1.3 collective-permute-start.12
  118.3 4.5 %collective-permute-start.13 = (f32[1,16,128]{2,1,0:T(8,128)S(1)}, f32[1,16,128]{2,1,0:T(8,128)S(1)}, u32[]{:S(2)}, u32[]{:S(2)}) collective-permute-start(f32[1,16,128]{2,1,0:T(8,128)S(1)} %get-tuple-element.111), channel_id=1, source_target_pairs={{0,16},{1,17},{2,18},{3,19},{4,20},{5,21},{6,22},{7,23},{8,24},{9,... | collective-permute-start | bytes 24584 | tf_op jit(solution)/shard_map/ppermute | solution.py:44
  122.9 1.3 collective-permute-done.13
  124.2 1.3 collective-permute-start.14
  125.5 4.8 %collective-permute-start.15 = (f32[10,1,128]{2,1,0:T(1,128)S(1)}, f32[10,1,128]{2,1,0:T(1,128)S(1)}, u32[]{:S(2)}, u32[]{:S(2)}) collective-permute-start(f32[10,1,128]{2,1,0:T(1,128)S(1)} %get-tuple-element.101), channel_id=1, source_target_pairs={{0,4},{4,8},{8,12},{1,5},{5,9},{9,13},{2,6},{6,10},{10,14},{3,7},{... | collective-permute-start | bytes 15368 | tf_op jit(solution)/shard_map/ppermute | solution.py:44
  130.3 1.3 collective-permute-done.15
  131.8 1.3 collective-permute-start.16
  133.1 3.3 collective-permute-start.17
  136.5 0.9 collective-permute-done.17
  138.8 48.9 %all-reduce.2 = (f32[64]{0:T(128)S(1)}, f32[]{:T(128)}, f32[]{:T(128)}) all-reduce(f32[64]{0:T(128)S(1)} %convolution_bitcast_fusion.24, f32[]{:T(128)} %get-tuple-element.10, f32[]{:T(128)} %get-tuple-element.8), channel_id=1, replica_groups=mesh['gx'=2,'gy'=4,'gz'=4] {'gx','gy','gz'}, use_global_device_ids=true, to_apply=%region_19.21 | all-reduce | flops 66 | bytes 528 | tf_op jit(solution)/shard_map/psum | solution.py:185
  189.0 1.3 collective-permute-start.18
  190.3 4.5 %collective-permute-start.19 = (f32[1,16,128]{2,1,0:T(8,128)S(1)}, f32[1,16,128]{2,1,0:T(8,128)S(1)}, u32[]{:S(2)}, u32[]{:S(2)}) collective-permute-start(f32[1,16,128]{2,1,0:T(8,128)S(1)} %slice.1129), channel_id=1, source_target_pairs={{0,16},{1,17},{2,18},{3,19},{4,20},{5,21},{6,22},{7,23},{8,24},{9,... | collective-permute-start | bytes 24584 | tf_op jit(solution)/shard_map/ppermute | solution.py:44
  194.9 1.3 collective-permute-done.19
  196.2 1.3 collective-permute-start.20
  197.5 4.5 %collective-permute-start.21 = (f32[10,1,128]{2,1,0:T(1,128)S(1)}, f32[10,1,128]{2,1,0:T(1,128)S(1)}, u32[]{:S(2)}, u32[]{:S(2)}) collective-permute-start(f32[10,1,128]{2,1,0:T(1,128)S(1)} %get-tuple-element.97), channel_id=1, source_target_pairs={{0,4},{4,8},{8,12},{1,5},{5,9},{9,13},{2,6},{6,10},{10,14},{3,7},{... | collective-permute-start | bytes 15368 | tf_op jit(solution)/shard_map/ppermute | solution.py:44
  204.2 1.3 collective-permute-start.22
  205.5 3.0 collective-permute-start.23
  208.6 0.9 collective-permute-done.23
  209.9 1.3 collective-permute-start.24
  211.2 4.5 %collective-permute-start.25 = (f32[1,16,128]{2,1,0:T(8,128)S(1)}, f32[1,16,128]{2,1,0:T(8,128)S(1)}, u32[]{:S(2)}, u32[]{:S(2)}) collective-permute-start(f32[1,16,128]{2,1,0:T(8,128)S(1)} %get-tuple-element.109), channel_id=1, source_target_pairs={{0,16},{1,17},{2,18},{3,19},{4,20},{5,21},{6,22},{7,23},{8,24},{9,... | collective-permute-start | bytes 24584 | tf_op jit(solution)/shard_map/ppermute | solution.py:44
  215.7 1.3 collective-permute-done.25
  217.1 1.3 collective-permute-start.26
  218.4 4.5 %collective-permute-start.27 = (f32[10,1,128]{2,1,0:T(1,128)S(1)}, f32[10,1,128]{2,1,0:T(1,128)S(1)}, u32[]{:S(2)}, u32[]{:S(2)}) collective-permute-start(f32[10,1,128]{2,1,0:T(1,128)S(1)} %get-tuple-element.93), channel_id=1, source_target_pairs={{0,4},{4,8},{8,12},{1,5},{5,9},{9,13},{2,6},{6,10},{10,14},{3,7},{... | collective-permute-start | bytes 15368 | tf_op jit(solution)/shard_map/ppermute | solution.py:44
  223.0 1.3 collective-permute-done.27
  224.4 1.3 collective-permute-start.28
  225.7 3.2 collective-permute-start.29
  229.0 0.9 collective-permute-done.29
  231.3 48.6 %all-reduce.1 = (f32[]{:T(128)}, f32[]{:T(128)}, f32[64]{0:T(128)S(1)}) all-reduce(f32[]{:T(128)} %get-tuple-element.7, f32[]{:T(128)} %get-tuple-element.6, f32[64]{0:T(128)S(1)} %convolution_bitcast_fusion.22), channel_id=1, replica_groups=mesh['gx'=2,'gy'=4,'gz'=4] {'gx','gy','gz'}, use_global_device_ids=true, to_apply=%region_22.24 | all-reduce | flops 66 | bytes 528 | tf_op jit(solution)/shard_map/psum | solution.py:185
  281.3 1.3 collective-permute-start.36
  282.6 4.5 %collective-permute-start.37 = (f32[1,16,128]{2,1,0:T(8,128)S(1)}, f32[1,16,128]{2,1,0:T(8,128)S(1)}, u32[]{:S(2)}, u32[]{:S(2)}) collective-permute-start(f32[1,16,128]{2,1,0:T(8,128)S(1)} %slice.1200), channel_id=1, source_target_pairs={{0,16},{1,17},{2,18},{3,19},{4,20},{5,21},{6,22},{7,23},{8,24},{9,... | collective-permute-start | bytes 24584 | tf_op jit(solution)/shard_map/ppermute | solution.py:44
  291.7 1.3 collective-permute-start.30
  293.0 4.5 %collective-permute-start.31 = (f32[1,16,128]{2,1,0:T(8,128)S(1)}, f32[1,16,128]{2,1,0:T(8,128)S(1)}, u32[]{:S(2)}, u32[]{:S(2)}) collective-permute-start(f32[1,16,128]{2,1,0:T(8,128)S(1)} %get-tuple-element.107), channel_id=1, source_target_pairs={{0,16},{1,17},{2,18},{3,19},{4,20},{5,21},{6,22},{7,23},{8,24},{9,... | collective-permute-start | bytes 24584 | tf_op jit(solution)/shard_map/ppermute | solution.py:44
  297.6 1.3 collective-permute-start.38
  298.9 4.5 %collective-permute-start.39 = (f32[10,1,128]{2,1,0:T(1,128)S(1)}, f32[10,1,128]{2,1,0:T(1,128)S(1)}, u32[]{:S(2)}, u32[]{:S(2)}) collective-permute-start(f32[10,1,128]{2,1,0:T(1,128)S(1)} %get-tuple-element.85), channel_id=1, source_target_pairs={{0,4},{4,8},{8,12},{1,5},{5,9},{9,13},{2,6},{6,10},{10,14},{3,7},{... | collective-permute-start | bytes 15368 | tf_op jit(solution)/shard_map/ppermute | solution.py:44
  303.5 1.3 collective-permute-start.32
  304.8 4.5 %collective-permute-start.33 = (f32[10,1,128]{2,1,0:T(1,128)S(1)}, f32[10,1,128]{2,1,0:T(1,128)S(1)}, u32[]{:S(2)}, u32[]{:S(2)}) collective-permute-start(f32[10,1,128]{2,1,0:T(1,128)S(1)} %get-tuple-element.89), channel_id=1, source_target_pairs={{0,4},{4,8},{8,12},{1,5},{5,9},{9,13},{2,6},{6,10},{10,14},{3,7},{... | collective-permute-start | bytes 15368 | tf_op jit(solution)/shard_map/ppermute | solution.py:44
  309.5 1.3 collective-permute-start.40
  310.8 3.0 collective-permute-start.41
  314.0 1.3 collective-permute-start.34
  315.3 4.7 %collective-permute-start.35 = (f32[10,18,1]{2,1,0:T(8,128)S(1)}, f32[10,18,1]{2,1,0:T(8,128)S(1)}, u32[]{:S(2)}, u32[]{:S(2)}) collective-permute-start(f32[10,18,1]{2,1,0:T(8,128)S(1)} %get-tuple-element.61), channel_id=1, source_target_pairs={{0,1},{1,2},{2,3},{4,5},{5,6},{6,7},{8,9},{9,10},{10,11},{12,13},{... | collective-permute-start | bytes 2168 | tf_op jit(solution)/shard_map/ppermute | solution.py:44
  321.7 40.9 %psum.71 = f32[64]{0:T(128)S(1)} all-reduce(f32[64]{0:T(128)S(1)} %convolution_bitcast_fusion.21), channel_id=1, replica_groups=mesh['gx'=2,'gy'=4,'gz'=4] {'gx','gy','gz'}, use_global_device_ids=true, to_apply=%region_31.33 | all-reduce | flops 64 | bytes 512 | tf_op jit(solution)/shard_map/psum | solution.py:171
  (216 shorter events, 28.7 us)
Async XLA Ops:
  0.6 10.1 %copy-start = (f32[8,16,128]{2,1,0:T(8,128)S(1)}, f32[8,16,128]{2,1,0:T(8,128)}, u32[]{:S(2)}) copy-start(f32[8,16,128]{2,1,0:T(8,128)} %param.7) | copy-start | bytes 196612
  0.6 10.3 %copy-start.1 = (s32[2,4,8]{2,1,0:T(4,128)S(1)}, s32[2,4,8]{2,1,0:T(4,128)}, u32[]{:S(2)}) copy-start(s32[2,4,8]{2,1,0:T(4,128)} %param.11) | copy-start | bytes 772
  4.2 7.1 %collective-permute-start = (f32[6,1,16,128]{3,2,1,0:T(8,128)S(1)}, f32[6,1,16,128]{3,2,1,0:T(8,128)S(1)}, u32[]{:S(2)}, u32[]{:S(2)}) collective-permute-start(f32[6,1,16,128]{3,2,1,0:T(8,128)S(1)} %get-tuple-element.39), channel_id=1, source_target_pairs={{0,16},{1,17},{2,18},{3,19},{4,20},{5,21},{6,22},{7,23},{8,24},{9,... | collective-permute-start | bytes 147464 | tf_op jit(solution)/shard_map/ppermute | solution.py:44
  9.1 6.0 %collective-permute-start.1 = (f32[6,1,16,128]{3,2,1,0:T(8,128)S(1)}, f32[6,1,16,128]{3,2,1,0:T(8,128)S(1)}, u32[]{:S(2)}, u32[]{:S(2)}) collective-permute-start(f32[6,1,16,128]{3,2,1,0:T(8,128)S(1)} %get-tuple-element.40), channel_id=1, source_target_pairs={{16,0},{17,1},{18,2},{19,3},{20,4},{21,5},{22,6},{23,7},{24,8},{25... | collective-permute-start | bytes 147464 | tf_op jit(solution)/shard_map/ppermute | solution.py:46
  15.1 5.0 %collective-permute-start.2 = (f32[6,10,1,128]{3,2,1,0:T(1,128)S(1)}, f32[6,10,1,128]{3,2,1,0:T(1,128)S(1)}, u32[]{:S(2)}, u32[]{:S(2)}) collective-permute-start(f32[6,10,1,128]{3,2,1,0:T(1,128)S(1)} %get-tuple-element.37), channel_id=1, source_target_pairs={{0,4},{4,8},{8,12},{1,5},{5,9},{9,13},{2,6},{6,10},{10,14},{3,7},{... | collective-permute-start | bytes 92168 | tf_op jit(solution)/shard_map/ppermute | solution.py:44
  18.6 5.8 %collective-permute-start.3 = (f32[6,10,1,128]{3,2,1,0:T(1,128)S(1)}, f32[6,10,1,128]{3,2,1,0:T(1,128)S(1)}, u32[]{:S(2)}, u32[]{:S(2)}) collective-permute-start(f32[6,10,1,128]{3,2,1,0:T(1,128)S(1)} %get-tuple-element.38), channel_id=1, source_target_pairs={{4,0},{8,4},{12,8},{5,1},{9,5},{13,9},{6,2},{10,6},{14,10},{7,3},{... | collective-permute-start | bytes 92168 | tf_op jit(solution)/shard_map/ppermute | solution.py:46
  25.2 3.1 collective-permute-start.4
  27.0 4.8 %collective-permute-start.5 = (f32[6,10,18,1]{2,3,1,0:T(1,128)S(1)}, f32[6,10,18,1]{2,3,1,0:T(1,128)S(1)}, u32[]{:S(2)}, u32[]{:S(2)}) collective-permute-start(f32[6,10,18,1]{2,3,1,0:T(1,128)S(1)} %copy.84), channel_id=1, source_target_pairs={{1,0},{2,1},{3,2},{5,4},{6,5},{7,6},{9,8},{10,9},{11,10},{13,12},{... | collective-permute-start | bytes 12968 | tf_op jit(solution)/shard_map/ppermute | solution.py:46
  96.8 5.9 %collective-permute-start.6 = (f32[1,16,128]{2,1,0:T(8,128)S(1)}, f32[1,16,128]{2,1,0:T(8,128)S(1)}, u32[]{:S(2)}, u32[]{:S(2)}) collective-permute-start(f32[1,16,128]{2,1,0:T(8,128)S(1)} %slice.1082), channel_id=1, source_target_pairs={{16,0},{17,1},{18,2},{19,3},{20,4},{21,5},{22,6},{23,7},{24,8},{25... | collective-permute-start | bytes 24584 | tf_op jit(solution)/shard_map/ppermute | solution.py:46
  98.1 5.9 %collective-permute-start.7 = (f32[1,16,128]{2,1,0:T(8,128)S(1)}, f32[1,16,128]{2,1,0:T(8,128)S(1)}, u32[]{:S(2)}, u32[]{:S(2)}) collective-permute-start(f32[1,16,128]{2,1,0:T(8,128)S(1)} %slice.1082), channel_id=1, source_target_pairs={{0,16},{1,17},{2,18},{3,19},{4,20},{5,21},{6,22},{7,23},{8,24},{9,... | collective-permute-start | bytes 24584 | tf_op jit(solution)/shard_map/ppermute | solution.py:44
  104.0 5.9 %collective-permute-start.8 = (f32[10,1,128]{2,1,0:T(1,128)S(1)}, f32[10,1,128]{2,1,0:T(1,128)S(1)}, u32[]{:S(2)}, u32[]{:S(2)}) collective-permute-start(f32[10,1,128]{2,1,0:T(1,128)S(1)} %get-tuple-element.106), channel_id=1, source_target_pairs={{4,0},{8,4},{12,8},{5,1},{9,5},{13,9},{6,2},{10,6},{14,10},{7,3},{... | collective-permute-start | bytes 15368 | tf_op jit(solution)/shard_map/ppermute | solution.py:46
  105.3 5.9 %collective-permute-start.9 = (f32[10,1,128]{2,1,0:T(1,128)S(1)}, f32[10,1,128]{2,1,0:T(1,128)S(1)}, u32[]{:S(2)}, u32[]{:S(2)}) collective-permute-start(f32[10,1,128]{2,1,0:T(1,128)S(1)} %get-tuple-element.105), channel_id=1, source_target_pairs={{0,4},{4,8},{8,12},{1,5},{5,9},{9,13},{2,6},{6,10},{10,14},{3,7},{... | collective-permute-start | bytes 15368 | tf_op jit(solution)/shard_map/ppermute | solution.py:44
  111.3 4.4 %collective-permute-start.10 = (f32[10,18,1]{2,1,0:T(8,128)S(1)}, f32[10,18,1]{2,1,0:T(8,128)S(1)}, u32[]{:S(2)}, u32[]{:S(2)}) collective-permute-start(f32[10,18,1]{2,1,0:T(8,128)S(1)} %get-tuple-element.70), channel_id=1, source_target_pairs={{1,0},{2,1},{3,2},{5,4},{6,5},{7,6},{9,8},{10,9},{11,10},{13,12},{... | collective-permute-start | bytes 2168 | tf_op jit(solution)/shard_map/ppermute | solution.py:46
  112.6 4.0 %collective-permute-start.11 = (f32[10,18,1]{2,1,0:T(8,128)S(1)}, f32[10,18,1]{2,1,0:T(8,128)S(1)}, u32[]{:S(2)}, u32[]{:S(2)}) collective-permute-start(f32[10,18,1]{2,1,0:T(8,128)S(1)} %get-tuple-element.69), channel_id=1, source_target_pairs={{0,1},{1,2},{2,3},{4,5},{5,6},{6,7},{8,9},{9,10},{10,11},{12,13},{... | collective-permute-start | bytes 2168 | tf_op jit(solution)/shard_map/ppermute | solution.py:44
  117.0 5.9 %collective-permute-start.12 = (f32[1,16,128]{2,1,0:T(8,128)S(1)}, f32[1,16,128]{2,1,0:T(8,128)S(1)}, u32[]{:S(2)}, u32[]{:S(2)}) collective-permute-start(f32[1,16,128]{2,1,0:T(8,128)S(1)} %get-tuple-element.112), channel_id=1, source_target_pairs={{16,0},{17,1},{18,2},{19,3},{20,4},{21,5},{22,6},{23,7},{24,8},{25... | collective-permute-start | bytes 24584 | tf_op jit(solution)/shard_map/ppermute | solution.py:46
  118.3 5.9 %collective-permute-start.13 = (f32[1,16,128]{2,1,0:T(8,128)S(1)}, f32[1,16,128]{2,1,0:T(8,128)S(1)}, u32[]{:S(2)}, u32[]{:S(2)}) collective-permute-start(f32[1,16,128]{2,1,0:T(8,128)S(1)} %get-tuple-element.111), channel_id=1, source_target_pairs={{0,16},{1,17},{2,18},{3,19},{4,20},{5,21},{6,22},{7,23},{8,24},{9,... | collective-permute-start | bytes 24584 | tf_op jit(solution)/shard_map/ppermute | solution.py:44
  124.2 6.1 %collective-permute-start.14 = (f32[10,1,128]{2,1,0:T(1,128)S(1)}, f32[10,1,128]{2,1,0:T(1,128)S(1)}, u32[]{:S(2)}, u32[]{:S(2)}) collective-permute-start(f32[10,1,128]{2,1,0:T(1,128)S(1)} %get-tuple-element.102), channel_id=1, source_target_pairs={{4,0},{8,4},{12,8},{5,1},{9,5},{13,9},{6,2},{10,6},{14,10},{7,3},{... | collective-permute-start | bytes 15368 | tf_op jit(solution)/shard_map/ppermute | solution.py:46
  125.5 6.1 %collective-permute-start.15 = (f32[10,1,128]{2,1,0:T(1,128)S(1)}, f32[10,1,128]{2,1,0:T(1,128)S(1)}, u32[]{:S(2)}, u32[]{:S(2)}) collective-permute-start(f32[10,1,128]{2,1,0:T(1,128)S(1)} %get-tuple-element.101), channel_id=1, source_target_pairs={{0,4},{4,8},{8,12},{1,5},{5,9},{9,13},{2,6},{6,10},{10,14},{3,7},{... | collective-permute-start | bytes 15368 | tf_op jit(solution)/shard_map/ppermute | solution.py:44
  131.8 4.7 %collective-permute-start.16 = (f32[10,18,1]{2,1,0:T(8,128)S(1)}, f32[10,18,1]{2,1,0:T(8,128)S(1)}, u32[]{:S(2)}, u32[]{:S(2)}) collective-permute-start(f32[10,18,1]{2,1,0:T(8,128)S(1)} %get-tuple-element.68), channel_id=1, source_target_pairs={{1,0},{2,1},{3,2},{5,4},{6,5},{7,6},{9,8},{10,9},{11,10},{13,12},{... | collective-permute-start | bytes 2168 | tf_op jit(solution)/shard_map/ppermute | solution.py:46
  133.1 4.3 %collective-permute-start.17 = (f32[10,18,1]{2,1,0:T(8,128)S(1)}, f32[10,18,1]{2,1,0:T(8,128)S(1)}, u32[]{:S(2)}, u32[]{:S(2)}) collective-permute-start(f32[10,18,1]{2,1,0:T(8,128)S(1)} %get-tuple-element.67), channel_id=1, source_target_pairs={{0,1},{1,2},{2,3},{4,5},{5,6},{6,7},{8,9},{9,10},{10,11},{12,13},{... | collective-permute-start | bytes 2168 | tf_op jit(solution)/shard_map/ppermute | solution.py:44
  189.0 5.8 %collective-permute-start.18 = (f32[1,16,128]{2,1,0:T(8,128)S(1)}, f32[1,16,128]{2,1,0:T(8,128)S(1)}, u32[]{:S(2)}, u32[]{:S(2)}) collective-permute-start(f32[1,16,128]{2,1,0:T(8,128)S(1)} %slice.1129), channel_id=1, source_target_pairs={{16,0},{17,1},{18,2},{19,3},{20,4},{21,5},{22,6},{23,7},{24,8},{25... | collective-permute-start | bytes 24584 | tf_op jit(solution)/shard_map/ppermute | solution.py:46
  190.3 5.9 %collective-permute-start.19 = (f32[1,16,128]{2,1,0:T(8,128)S(1)}, f32[1,16,128]{2,1,0:T(8,128)S(1)}, u32[]{:S(2)}, u32[]{:S(2)}) collective-permute-start(f32[1,16,128]{2,1,0:T(8,128)S(1)} %slice.1129), channel_id=1, source_target_pairs={{0,16},{1,17},{2,18},{3,19},{4,20},{5,21},{6,22},{7,23},{8,24},{9,... | collective-permute-start | bytes 24584 | tf_op jit(solution)/shard_map/ppermute | solution.py:44
  196.2 7.8 %collective-permute-start.20 = (f32[10,1,128]{2,1,0:T(1,128)S(1)}, f32[10,1,128]{2,1,0:T(1,128)S(1)}, u32[]{:S(2)}, u32[]{:S(2)}) collective-permute-start(f32[10,1,128]{2,1,0:T(1,128)S(1)} %get-tuple-element.98), channel_id=1, source_target_pairs={{4,0},{8,4},{12,8},{5,1},{9,5},{13,9},{6,2},{10,6},{14,10},{7,3},{... | collective-permute-start | bytes 15368 | tf_op jit(solution)/shard_map/ppermute | solution.py:46
  197.5 6.5 %collective-permute-start.21 = (f32[10,1,128]{2,1,0:T(1,128)S(1)}, f32[10,1,128]{2,1,0:T(1,128)S(1)}, u32[]{:S(2)}, u32[]{:S(2)}) collective-permute-start(f32[10,1,128]{2,1,0:T(1,128)S(1)} %get-tuple-element.97), channel_id=1, source_target_pairs={{0,4},{4,8},{8,12},{1,5},{5,9},{9,13},{2,6},{6,10},{10,14},{3,7},{... | collective-permute-start | bytes 15368 | tf_op jit(solution)/shard_map/ppermute | solution.py:44
  204.2 4.4 %collective-permute-start.22 = (f32[10,18,1]{2,1,0:T(8,128)S(1)}, f32[10,18,1]{2,1,0:T(8,128)S(1)}, u32[]{:S(2)}, u32[]{:S(2)}) collective-permute-start(f32[10,18,1]{2,1,0:T(8,128)S(1)} %get-tuple-element.66), channel_id=1, source_target_pairs={{1,0},{2,1},{3,2},{5,4},{6,5},{7,6},{9,8},{10,9},{11,10},{13,12},{... | collective-permute-start | bytes 2168 | tf_op jit(solution)/shard_map/ppermute | solution.py:46
  205.5 4.0 %collective-permute-start.23 = (f32[10,18,1]{2,1,0:T(8,128)S(1)}, f32[10,18,1]{2,1,0:T(8,128)S(1)}, u32[]{:S(2)}, u32[]{:S(2)}) collective-permute-start(f32[10,18,1]{2,1,0:T(8,128)S(1)} %get-tuple-element.65), channel_id=1, source_target_pairs={{0,1},{1,2},{2,3},{4,5},{5,6},{6,7},{8,9},{9,10},{10,11},{12,13},{... | collective-permute-start | bytes 2168 | tf_op jit(solution)/shard_map/ppermute | solution.py:44
  209.9 5.9 %collective-permute-start.24 = (f32[1,16,128]{2,1,0:T(8,128)S(1)}, f32[1,16,128]{2,1,0:T(8,128)S(1)}, u32[]{:S(2)}, u32[]{:S(2)}) collective-permute-start(f32[1,16,128]{2,1,0:T(8,128)S(1)} %get-tuple-element.110), channel_id=1, source_target_pairs={{16,0},{17,1},{18,2},{19,3},{20,4},{21,5},{22,6},{23,7},{24,8},{25... | collective-permute-start | bytes 24584 | tf_op jit(solution)/shard_map/ppermute | solution.py:46
  211.2 5.9 %collective-permute-start.25 = (f32[1,16,128]{2,1,0:T(8,128)S(1)}, f32[1,16,128]{2,1,0:T(8,128)S(1)}, u32[]{:S(2)}, u32[]{:S(2)}) collective-permute-start(f32[1,16,128]{2,1,0:T(8,128)S(1)} %get-tuple-element.109), channel_id=1, source_target_pairs={{0,16},{1,17},{2,18},{3,19},{4,20},{5,21},{6,22},{7,23},{8,24},{9,... | collective-permute-start | bytes 24584 | tf_op jit(solution)/shard_map/ppermute | solution.py:44
  217.1 5.9 %collective-permute-start.26 = (f32[10,1,128]{2,1,0:T(1,128)S(1)}, f32[10,1,128]{2,1,0:T(1,128)S(1)}, u32[]{:S(2)}, u32[]{:S(2)}) collective-permute-start(f32[10,1,128]{2,1,0:T(1,128)S(1)} %get-tuple-element.94), channel_id=1, source_target_pairs={{4,0},{8,4},{12,8},{5,1},{9,5},{13,9},{6,2},{10,6},{14,10},{7,3},{... | collective-permute-start | bytes 15368 | tf_op jit(solution)/shard_map/ppermute | solution.py:46
  218.4 5.9 %collective-permute-start.27 = (f32[10,1,128]{2,1,0:T(1,128)S(1)}, f32[10,1,128]{2,1,0:T(1,128)S(1)}, u32[]{:S(2)}, u32[]{:S(2)}) collective-permute-start(f32[10,1,128]{2,1,0:T(1,128)S(1)} %get-tuple-element.93), channel_id=1, source_target_pairs={{0,4},{4,8},{8,12},{1,5},{5,9},{9,13},{2,6},{6,10},{10,14},{3,7},{... | collective-permute-start | bytes 15368 | tf_op jit(solution)/shard_map/ppermute | solution.py:44
  224.4 4.6 %collective-permute-start.28 = (f32[10,18,1]{2,1,0:T(8,128)S(1)}, f32[10,18,1]{2,1,0:T(8,128)S(1)}, u32[]{:S(2)}, u32[]{:S(2)}) collective-permute-start(f32[10,18,1]{2,1,0:T(8,128)S(1)} %get-tuple-element.64), channel_id=1, source_target_pairs={{1,0},{2,1},{3,2},{5,4},{6,5},{7,6},{9,8},{10,9},{11,10},{13,12},{... | collective-permute-start | bytes 2168 | tf_op jit(solution)/shard_map/ppermute | solution.py:46
  225.7 4.2 %collective-permute-start.29 = (f32[10,18,1]{2,1,0:T(8,128)S(1)}, f32[10,18,1]{2,1,0:T(8,128)S(1)}, u32[]{:S(2)}, u32[]{:S(2)}) collective-permute-start(f32[10,18,1]{2,1,0:T(8,128)S(1)} %get-tuple-element.63), channel_id=1, source_target_pairs={{0,1},{1,2},{2,3},{4,5},{5,6},{6,7},{8,9},{9,10},{10,11},{12,13},{... | collective-permute-start | bytes 2168 | tf_op jit(solution)/shard_map/ppermute | solution.py:44
  281.3 16.3 %collective-permute-start.36 = (f32[1,16,128]{2,1,0:T(8,128)S(1)}, f32[1,16,128]{2,1,0:T(8,128)S(1)}, u32[]{:S(2)}, u32[]{:S(2)}) collective-permute-start(f32[1,16,128]{2,1,0:T(8,128)S(1)} %slice.1200), channel_id=1, source_target_pairs={{16,0},{17,1},{18,2},{19,3},{20,4},{21,5},{22,6},{23,7},{24,8},{25... | collective-permute-start | bytes 24584 | tf_op jit(solution)/shard_map/ppermute | solution.py:46
  282.6 15.0 %collective-permute-start.37 = (f32[1,16,128]{2,1,0:T(8,128)S(1)}, f32[1,16,128]{2,1,0:T(8,128)S(1)}, u32[]{:S(2)}, u32[]{:S(2)}) collective-permute-start(f32[1,16,128]{2,1,0:T(8,128)S(1)} %slice.1200), channel_id=1, source_target_pairs={{0,16},{1,17},{2,18},{3,19},{4,20},{5,21},{6,22},{7,23},{8,24},{9,... | collective-permute-start | bytes 24584 | tf_op jit(solution)/shard_map/ppermute | solution.py:44
  291.7 11.8 %collective-permute-start.30 = (f32[1,16,128]{2,1,0:T(8,128)S(1)}, f32[1,16,128]{2,1,0:T(8,128)S(1)}, u32[]{:S(2)}, u32[]{:S(2)}) collective-permute-start(f32[1,16,128]{2,1,0:T(8,128)S(1)} %get-tuple-element.108), channel_id=1, source_target_pairs={{16,0},{17,1},{18,2},{19,3},{20,4},{21,5},{22,6},{23,7},{24,8},{25... | collective-permute-start | bytes 24584 | tf_op jit(solution)/shard_map/ppermute | solution.py:46
  293.0 10.5 %collective-permute-start.31 = (f32[1,16,128]{2,1,0:T(8,128)S(1)}, f32[1,16,128]{2,1,0:T(8,128)S(1)}, u32[]{:S(2)}, u32[]{:S(2)}) collective-permute-start(f32[1,16,128]{2,1,0:T(8,128)S(1)} %get-tuple-element.107), channel_id=1, source_target_pairs={{0,16},{1,17},{2,18},{3,19},{4,20},{5,21},{6,22},{7,23},{8,24},{9,... | collective-permute-start | bytes 24584 | tf_op jit(solution)/shard_map/ppermute | solution.py:44
  297.6 11.8 %collective-permute-start.38 = (f32[10,1,128]{2,1,0:T(1,128)S(1)}, f32[10,1,128]{2,1,0:T(1,128)S(1)}, u32[]{:S(2)}, u32[]{:S(2)}) collective-permute-start(f32[10,1,128]{2,1,0:T(1,128)S(1)} %get-tuple-element.86), channel_id=1, source_target_pairs={{4,0},{8,4},{12,8},{5,1},{9,5},{13,9},{6,2},{10,6},{14,10},{7,3},{... | collective-permute-start | bytes 15368 | tf_op jit(solution)/shard_map/ppermute | solution.py:46
  298.9 10.5 %collective-permute-start.39 = (f32[10,1,128]{2,1,0:T(1,128)S(1)}, f32[10,1,128]{2,1,0:T(1,128)S(1)}, u32[]{:S(2)}, u32[]{:S(2)}) collective-permute-start(f32[10,1,128]{2,1,0:T(1,128)S(1)} %get-tuple-element.85), channel_id=1, source_target_pairs={{0,4},{4,8},{8,12},{1,5},{5,9},{9,13},{2,6},{6,10},{10,14},{3,7},{... | collective-permute-start | bytes 15368 | tf_op jit(solution)/shard_map/ppermute | solution.py:44
  303.5 10.3 %collective-permute-start.32 = (f32[10,1,128]{2,1,0:T(1,128)S(1)}, f32[10,1,128]{2,1,0:T(1,128)S(1)}, u32[]{:S(2)}, u32[]{:S(2)}) collective-permute-start(f32[10,1,128]{2,1,0:T(1,128)S(1)} %get-tuple-element.90), channel_id=1, source_target_pairs={{4,0},{8,4},{12,8},{5,1},{9,5},{13,9},{6,2},{10,6},{14,10},{7,3},{... | collective-permute-start | bytes 15368 | tf_op jit(solution)/shard_map/ppermute | solution.py:46
  304.8 9.1 %collective-permute-start.33 = (f32[10,1,128]{2,1,0:T(1,128)S(1)}, f32[10,1,128]{2,1,0:T(1,128)S(1)}, u32[]{:S(2)}, u32[]{:S(2)}) collective-permute-start(f32[10,1,128]{2,1,0:T(1,128)S(1)} %get-tuple-element.89), channel_id=1, source_target_pairs={{0,4},{4,8},{8,12},{1,5},{5,9},{9,13},{2,6},{6,10},{10,14},{3,7},{... | collective-permute-start | bytes 15368 | tf_op jit(solution)/shard_map/ppermute | solution.py:44
  309.5 54.4 %collective-permute-start.40 = (f32[10,18,1]{2,1,0:T(8,128)S(1)}, f32[10,18,1]{2,1,0:T(8,128)S(1)}, u32[]{:S(2)}, u32[]{:S(2)}) collective-permute-start(f32[10,18,1]{2,1,0:T(8,128)S(1)} %get-tuple-element.60), channel_id=1, source_target_pairs={{1,0},{2,1},{3,2},{5,4},{6,5},{7,6},{9,8},{10,9},{11,10},{13,12},{... | collective-permute-start | bytes 2168 | tf_op jit(solution)/shard_map/ppermute | solution.py:46
  310.8 53.1 %collective-permute-start.41 = (f32[10,18,1]{2,1,0:T(8,128)S(1)}, f32[10,18,1]{2,1,0:T(8,128)S(1)}, u32[]{:S(2)}, u32[]{:S(2)}) collective-permute-start(f32[10,18,1]{2,1,0:T(8,128)S(1)} %get-tuple-element.59), channel_id=1, source_target_pairs={{0,1},{1,2},{2,3},{4,5},{5,6},{6,7},{8,9},{9,10},{10,11},{12,13},{... | collective-permute-start | bytes 2168 | tf_op jit(solution)/shard_map/ppermute | solution.py:44
  314.0 6.0 %collective-permute-start.34 = (f32[10,18,1]{2,1,0:T(8,128)S(1)}, f32[10,18,1]{2,1,0:T(8,128)S(1)}, u32[]{:S(2)}, u32[]{:S(2)}) collective-permute-start(f32[10,18,1]{2,1,0:T(8,128)S(1)} %get-tuple-element.62), channel_id=1, source_target_pairs={{1,0},{2,1},{3,2},{5,4},{6,5},{7,6},{9,8},{10,9},{11,10},{13,12},{... | collective-permute-start | bytes 2168 | tf_op jit(solution)/shard_map/ppermute | solution.py:46
  315.3 5.6 %collective-permute-start.35 = (f32[10,18,1]{2,1,0:T(8,128)S(1)}, f32[10,18,1]{2,1,0:T(8,128)S(1)}, u32[]{:S(2)}, u32[]{:S(2)}) collective-permute-start(f32[10,18,1]{2,1,0:T(8,128)S(1)} %get-tuple-element.61), channel_id=1, source_target_pairs={{0,1},{1,2},{2,3},{4,5},{5,6},{6,7},{8,9},{9,10},{10,11},{12,13},{... | collective-permute-start | bytes 2168 | tf_op jit(solution)/shard_map/ppermute | solution.py:44
where the time goes:
time: 367 us; the launch traced here: 365 us
  blocking collectives  179 us (49%)
  starting transfers between devices  112 us (31%)
  waiting for transfers between devices  25.1 us (7%)
  other arithmetic  22.3 us (6%)
  matrix products  13.4 us (4%)
  between operations  8.31 us (2%)
  local copies, waits for them, and re-layouts  5.09 us (1%)
    psum x2, blocking collectives, joint_terms(): lax.psum((restrict(product), jnp.sum(field * field), jnp.sum(field * prod...  97.5 us
    ppermute x21, starting transfers between devices, padded_2(): lax.ppermute(tail, axis, [(i, (i + 1) % count) for i in range(ends)])  84.8 us
    psum x1, blocking collectives, coarse_solve(): projected = lax.psum(restrict(field), ('gx', 'gy', 'gz'))  40.9 us
    psum x1, blocking collectives, body(): coarse = lax.psum(jnp.diag(diagonal_terms) - coupling, ('gx', 'gy', 'gz'))  40.4 us
    ppermute x21, starting transfers between devices, padded_2(): lax.ppermute(head, axis, [((i + 1) % count, i) for i in range(ends)])  27.1 us
    ppermute x21, waiting for transfers between devices, padded_2(): lax.ppermute(tail, axis, [(i, (i + 1) % count) for i in range(ends)])  14.1 us
    ppermute x21, waiting for transfers between devices, padded_2(): lax.ppermute(head, axis, [((i + 1) % count, i) for i in range(ends)])  11 us
    dot_general x54, matrix products, body(): jnp.einsum('xyz,xa,yb,zjc->jabc', weight, reach_onehot(CX, step_x), reach...  8.59 us
  transfers between devices with their start and end apart: 42, of which 16 were waited for; matrix products, arithmetic and copies ran while one was open for 1% of the time, Pallas kernels for 0%

commit v1 on v0

--- a/solution.py
+++ b/solution.py
@@ -151,7 +151,9 @@
         class_onehot(neighbours, COARSE),
         precision=highest,
     )
-    coarse = lax.psum(jnp.diag(diagonal_terms) - coupling, ("gx", "gy", "gz"))
+    part = jnp.diag(diagonal_terms) - coupling
+    terms = lax.all_gather(part, ("gx", "gy", "gz"), axis=0, tiled=False)
+    coarse = terms.sum(axis=0)
     coarse = 0.5 * (coarse + coarse.T)
     factor_lower = jnp.linalg.cholesky(coarse)
 

time: 367 us -> 408 us (1.11)
  blocking collectives: 179 us -> 223 us
    all_gather x0 -> x1, blocking collectives: none -> 44.6 us  [body(): terms = lax.all_gather(part, ('gx', 'gy', 'gz'), axis=0, tiled=False)]
    psum x1 -> x2, blocking collectives: 40.9 us -> 82.7 us  [coarse_solve(): projected = lax.psum(restrict(field), ('gx', 'gy', 'gz'))]
    psum x1 -> x0, blocking collectives: 40.4 us -> none  [body(): coarse = lax.psum(jnp.diag(diagonal_terms) - coupling, ('gx', 'gy', 'gz'))]
  transfers between devices with their start and end apart: 42 -> 42, of which waited for: 16 -> 15; matrix products, arithmetic and copies ran while one was open for 1% -> 1% of each run, Pallas kernels for 0% -> 0%
where the time goes in v1:
time: 408 us; the launch traced here: 406 us
  blocking collectives  223 us (55%)
  starting transfers between devices  112 us (27%)
  other arithmetic  22.5 us (6%)
  waiting for transfers between devices  21.9 us (5%)
  matrix products  13.4 us (3%)
  between operations  8.08 us (2%)
  local copies, waits for them, and re-layouts  5.02 us (1%)
    psum x2, blocking collectives, joint_terms(): lax.psum((restrict(product), jnp.sum(field * field), jnp.sum(field * prod...  95.9 us
    ppermute x21, starting transfers between devices, padded_2(): lax.ppermute(tail, axis, [(i, (i + 1) % count) for i in range(ends)])  84.6 us
    psum x2, blocking collectives, coarse_solve(): projected = lax.psum(restrict(field), ('gx', 'gy', 'gz'))  82.7 us
    all_gather x1, blocking collectives, body(): terms = lax.all_gather(part, ('gx', 'gy', 'gz'), axis=0, tiled=False)  44.6 us
    ppermute x21, starting transfers between devices, padded_2(): lax.ppermute(head, axis, [((i + 1) % count, i) for i in range(ends)])  27.1 us
    ppermute x21, waiting for transfers between devices, padded_2(): lax.ppermute(tail, axis, [(i, (i + 1) % count) for i in range(ends)])  13.9 us
    dot_general x54, matrix products, body(): jnp.einsum('xyz,xa,yb,zjc->jabc', weight, reach_onehot(CX, step_x), reach...  8.59 us
  transfers between devices with their start and end apart: 42, of which 15 were waited for; matrix products, arithmetic and copies ran while one was open for 1% of the time, Pallas kernels for 0%

profile of v1, /device:TPU:0, one launch (start us, length us, event | category | flops | bytes accessed | tf_op | source)
XLA Modules:
  0.0 405.8 jit_solution(12983472376259670186)
XLA Ops:
  0.6 0.9 slice_bitcast_fusion.11
  1.6 1.7 select_reduce_fusion
  4.2 4.9 %collective-permute-start = (f32[6,1,16,128]{3,2,1,0:T(8,128)S(1)}, f32[6,1,16,128]{3,2,1,0:T(8,128)S(1)}, u32[]{:S(2)}, u32[]{:S(2)}) collective-permute-start(f32[6,1,16,128]{3,2,1,0:T(8,128)S(1)} %get-tuple-element.37), channel_id=1, source_target_pairs={{0,16},{1,17},{2,18},{3,19},{4,20},{5,21},{6,22},{7,23},{8,24},{9,... | collective-permute-start | bytes 147464 | tf_op jit(solution)/shard_map/ppermute | solution.py:44
  9.1 1.3 collective-permute-start.1
  11.4 3.7 collective-permute-done.1
  15.1 3.5 collective-permute-start.2
  18.6 1.3 collective-permute-start.3
  20.2 4.2 %collective-permute-done.3 = f32[6,10,1,128]{3,2,1,0:T(1,128)S(1)} collective-permute-done((f32[6,10,1,128]{3,2,1,0:T(1,128)S(1)}, f32[6,10,1,128]{3,2,1,0:T(1,128)S(1)}, u32[]{:S(2)}, u32[]{:S(2)}) %collective-permute-start.3) | collective-permute-done | bytes 30752 | tf_op jit(solution)/shard_map/ppermute | solution.py:46
  25.2 1.3 collective-permute-start.4
  27.0 1.3 collective-permute-start.5
  28.3 42.0 %psum.56 = f32[64]{0:T(128)S(1)} all-reduce(f32[64]{0:T(128)S(1)} %convolution_bitcast_fusion.26), channel_id=1, replica_groups=mesh['gx'=2,'gy'=4,'gz'=4] {'gx','gy','gz'}, use_global_device_ids=true, to_apply=%region_12.13 | all-reduce | flops 64 | bytes 512 | tf_op jit(solution)/shard_map/psum | solution.py:173
  82.4 44.6 %all-gather = f32[2048,64]{1,0:T(8,128)S(1)} all-gather(f32[64,64]{1,0:T(8,128)S(1)} %convolution_subtract_fusion), channel_id=2, replica_groups=mesh['gx'=2,'gy'=4,'gz'=4] {'gx','gy','gz'}, dimensions={0}, use_global_device_ids=true | all-gather | bytes 540672 | tf_op jit(solution)/shard_map/all_gather | solution.py:155
  127.2 5.8 %cholesky.19 = f32[64,64]{1,0:T(8,128)S(1)} custom-call(f32[64,64]{1,0:T(8,128)S(1)} %fusion.263), custom_call_target="Cholesky" | custom-call | tf_op jit(solution)/shard_map/jit(cholesky)/cholesky | solution.py:158
  134.4 4.9 %custom-call.11 = f32[1,64,64]{1,2,0:T(8,128)S(1)} custom-call(f32[1,64,64]{2,1,0:T(8,128)S(1)} %fusion.251), custom_call_target="InvertDiagBlocksLowerTriangular" | custom-call | tf_op jit(solution)/shard_map/jit(_cho_solve)/triangular_solve | solution.py:174
  140.0 1.3 collective-permute-start.6
  141.3 4.5 %collective-permute-start.7 = (f32[1,16,128]{2,1,0:T(8,128)S(1)}, f32[1,16,128]{2,1,0:T(8,128)S(1)}, u32[]{:S(2)}, u32[]{:S(2)}) collective-permute-start(f32[1,16,128]{2,1,0:T(8,128)S(1)} %slice.1082), channel_id=1, source_target_pairs={{0,16},{1,17},{2,18},{3,19},{4,20},{5,21},{6,22},{7,23},{8,24},{9,... | collective-permute-start | bytes 24584 | tf_op jit(solution)/shard_map/ppermute | solution.py:44
  145.8 1.3 collective-permute-done.7
  147.2 1.3 collective-permute-start.8
  148.5 4.5 %collective-permute-start.9 = (f32[10,1,128]{2,1,0:T(1,128)S(1)}, f32[10,1,128]{2,1,0:T(1,128)S(1)}, u32[]{:S(2)}, u32[]{:S(2)}) collective-permute-start(f32[10,1,128]{2,1,0:T(1,128)S(1)} %get-tuple-element.103), channel_id=1, source_target_pairs={{0,4},{4,8},{8,12},{1,5},{5,9},{9,13},{2,6},{6,10},{10,14},{3,7},{... | collective-permute-start | bytes 15368 | tf_op jit(solution)/shard_map/ppermute | solution.py:44
  153.0 1.3 collective-permute-done.9
  154.5 1.3 collective-permute-start.10
  155.8 3.0 collective-permute-start.11
  158.9 0.9 collective-permute-done.11
  160.2 1.3 collective-permute-start.12
  161.5 4.5 %collective-permute-start.13 = (f32[1,16,128]{2,1,0:T(8,128)S(1)}, f32[1,16,128]{2,1,0:T(8,128)S(1)}, u32[]{:S(2)}, u32[]{:S(2)}) collective-permute-start(f32[1,16,128]{2,1,0:T(8,128)S(1)} %get-tuple-element.109), channel_id=1, source_target_pairs={{0,16},{1,17},{2,18},{3,19},{4,20},{5,21},{6,22},{7,23},{8,24},{9,... | collective-permute-start | bytes 24584 | tf_op jit(solution)/shard_map/ppermute | solution.py:44
  166.0 1.3 collective-permute-done.13
  167.4 1.3 collective-permute-start.14
  168.7 4.8 %collective-permute-start.15 = (f32[10,1,128]{2,1,0:T(1,128)S(1)}, f32[10,1,128]{2,1,0:T(1,128)S(1)}, u32[]{:S(2)}, u32[]{:S(2)}) collective-permute-start(f32[10,1,128]{2,1,0:T(1,128)S(1)} %get-tuple-element.99), channel_id=1, source_target_pairs={{0,4},{4,8},{8,12},{1,5},{5,9},{9,13},{2,6},{6,10},{10,14},{3,7},{... | collective-permute-start | bytes 15368 | tf_op jit(solution)/shard_map/ppermute | solution.py:44
  173.5 1.3 collective-permute-done.15
  175.0 1.3 collective-permute-start.16
  176.3 3.2 collective-permute-start.17
  181.7 47.2 %all-reduce.2 = (f32[64]{0:T(128)S(1)}, f32[]{:T(128)}, f32[]{:T(128)}) all-reduce(f32[64]{0:T(128)S(1)} %convolution_bitcast_fusion.24, f32[]{:T(128)} %get-tuple-element.10, f32[]{:T(128)} %get-tuple-element.8), channel_id=1, replica_groups=mesh['gx'=2,'gy'=4,'gz'=4] {'gx','gy','gz'}, use_global_device_ids=true, to_apply=%region_19.21 | all-reduce | flops 66 | bytes 528 | tf_op jit(solution)/shard_map/psum | solution.py:187
  230.1 1.3 collective-permute-start.18
  231.4 4.5 %collective-permute-start.19 = (f32[1,16,128]{2,1,0:T(8,128)S(1)}, f32[1,16,128]{2,1,0:T(8,128)S(1)}, u32[]{:S(2)}, u32[]{:S(2)}) collective-permute-start(f32[1,16,128]{2,1,0:T(8,128)S(1)} %slice.1129), channel_id=1, source_target_pairs={{0,16},{1,17},{2,18},{3,19},{4,20},{5,21},{6,22},{7,23},{8,24},{9,... | collective-permute-start | bytes 24584 | tf_op jit(solution)/shard_map/ppermute | solution.py:44
  236.0 1.3 collective-permute-done.19
  237.3 1.3 collective-permute-start.20
  238.6 4.5 %collective-permute-start.21 = (f32[10,1,128]{2,1,0:T(1,128)S(1)}, f32[10,1,128]{2,1,0:T(1,128)S(1)}, u32[]{:S(2)}, u32[]{:S(2)}) collective-permute-start(f32[10,1,128]{2,1,0:T(1,128)S(1)} %get-tuple-element.95), channel_id=1, source_target_pairs={{0,4},{4,8},{8,12},{1,5},{5,9},{9,13},{2,6},{6,10},{10,14},{3,7},{... | collective-permute-start | bytes 15368 | tf_op jit(solution)/shard_map/ppermute | solution.py:44
  245.2 1.3 collective-permute-start.22
  246.5 3.0 collective-permute-start.23
  249.6 0.9 collective-permute-done.23
  250.9 1.3 collective-permute-start.24
  252.2 4.5 %collective-permute-start.25 = (f32[1,16,128]{2,1,0:T(8,128)S(1)}, f32[1,16,128]{2,1,0:T(8,128)S(1)}, u32[]{:S(2)}, u32[]{:S(2)}) collective-permute-start(f32[1,16,128]{2,1,0:T(8,128)S(1)} %get-tuple-element.107), channel_id=1, source_target_pairs={{0,16},{1,17},{2,18},{3,19},{4,20},{5,21},{6,22},{7,23},{8,24},{9,... | collective-permute-start | bytes 24584 | tf_op jit(solution)/shard_map/ppermute | solution.py:44
  256.8 1.3 collective-permute-done.25
  258.1 1.3 collective-permute-start.26
  259.4 4.5 %collective-permute-start.27 = (f32[10,1,128]{2,1,0:T(1,128)S(1)}, f32[10,1,128]{2,1,0:T(1,128)S(1)}, u32[]{:S(2)}, u32[]{:S(2)}) collective-permute-start(f32[10,1,128]{2,1,0:T(1,128)S(1)} %get-tuple-element.91), channel_id=1, source_target_pairs={{0,4},{4,8},{8,12},{1,5},{5,9},{9,13},{2,6},{6,10},{10,14},{3,7},{... | collective-permute-start | bytes 15368 | tf_op jit(solution)/shard_map/ppermute | solution.py:44
  264.0 1.3 collective-permute-done.27
  265.4 1.3 collective-permute-start.28
  266.7 3.2 collective-permute-start.29
  270.0 0.9 collective-permute-done.29
  271.1 0.9 fusion.452
  272.4 48.7 %all-reduce.1 = (f32[]{:T(128)}, f32[]{:T(128)}, f32[64]{0:T(128)S(1)}) all-reduce(f32[]{:T(128)} %get-tuple-element.7, f32[]{:T(128)} %get-tuple-element.6, f32[64]{0:T(128)S(1)} %convolution_bitcast_fusion.22), channel_id=1, replica_groups=mesh['gx'=2,'gy'=4,'gz'=4] {'gx','gy','gz'}, use_global_device_ids=true, to_apply=%region_22.24 | all-reduce | flops 66 | bytes 528 | tf_op jit(solution)/shard_map/psum | solution.py:187
  322.5 1.3 collective-permute-start.36
  323.8 4.5 %collective-permute-start.37 = (f32[1,16,128]{2,1,0:T(8,128)S(1)}, f32[1,16,128]{2,1,0:T(8,128)S(1)}, u32[]{:S(2)}, u32[]{:S(2)}) collective-permute-start(f32[1,16,128]{2,1,0:T(8,128)S(1)} %slice.1200), channel_id=1, source_target_pairs={{0,16},{1,17},{2,18},{3,19},{4,20},{5,21},{6,22},{7,23},{8,24},{9,... | collective-permute-start | bytes 24584 | tf_op jit(solution)/shard_map/ppermute | solution.py:44
  332.8 1.3 collective-permute-start.30
  334.1 4.5 %collective-permute-start.31 = (f32[1,16,128]{2,1,0:T(8,128)S(1)}, f32[1,16,128]{2,1,0:T(8,128)S(1)}, u32[]{:S(2)}, u32[]{:S(2)}) collective-permute-start(f32[1,16,128]{2,1,0:T(8,128)S(1)} %get-tuple-element.105), channel_id=1, source_target_pairs={{0,16},{1,17},{2,18},{3,19},{4,20},{5,21},{6,22},{7,23},{8,24},{9,... | collective-permute-start | bytes 24584 | tf_op jit(solution)/shard_map/ppermute | solution.py:44
  338.7 1.3 collective-permute-start.38
  340.0 4.5 %collective-permute-start.39 = (f32[10,1,128]{2,1,0:T(1,128)S(1)}, f32[10,1,128]{2,1,0:T(1,128)S(1)}, u32[]{:S(2)}, u32[]{:S(2)}) collective-permute-start(f32[10,1,128]{2,1,0:T(1,128)S(1)} %get-tuple-element.83), channel_id=1, source_target_pairs={{0,4},{4,8},{8,12},{1,5},{5,9},{9,13},{2,6},{6,10},{10,14},{3,7},{... | collective-permute-start | bytes 15368 | tf_op jit(solution)/shard_map/ppermute | solution.py:44
  344.6 1.3 collective-permute-start.32
  345.9 4.5 %collective-permute-start.33 = (f32[10,1,128]{2,1,0:T(1,128)S(1)}, f32[10,1,128]{2,1,0:T(1,128)S(1)}, u32[]{:S(2)}, u32[]{:S(2)}) collective-permute-start(f32[10,1,128]{2,1,0:T(1,128)S(1)} %get-tuple-element.87), channel_id=1, source_target_pairs={{0,4},{4,8},{8,12},{1,5},{5,9},{9,13},{2,6},{6,10},{10,14},{3,7},{... | collective-permute-start | bytes 15368 | tf_op jit(solution)/shard_map/ppermute | solution.py:44
  350.6 1.3 collective-permute-start.40
  351.9 3.0 collective-permute-start.41
  355.1 1.3 collective-permute-start.34
  356.4 4.6 %collective-permute-start.35 = (f32[10,18,1]{2,1,0:T(8,128)S(1)}, f32[10,18,1]{2,1,0:T(8,128)S(1)}, u32[]{:S(2)}, u32[]{:S(2)}) collective-permute-start(f32[10,18,1]{2,1,0:T(8,128)S(1)} %get-tuple-element.59), channel_id=1, source_target_pairs={{0,1},{1,2},{2,3},{4,5},{5,6},{6,7},{8,9},{9,10},{10,11},{12,13},{... | collective-permute-start | bytes 2168 | tf_op jit(solution)/shard_map/ppermute | solution.py:44
  362.7 40.7 %psum.63 = f32[64]{0:T(128)S(1)} all-reduce(f32[64]{0:T(128)S(1)} %convolution_bitcast_fusion.21), channel_id=1, replica_groups=mesh['gx'=2,'gy'=4,'gz'=4] {'gx','gy','gz'}, use_global_device_ids=true, to_apply=%region_31.33 | all-reduce | flops 64 | bytes 512 | tf_op jit(solution)/shard_map/psum | solution.py:173
  (216 shorter events, 28.6 us)
Async XLA Ops:
  0.6 10.1 %copy-start = (f32[8,16,128]{2,1,0:T(8,128)S(1)}, f32[8,16,128]{2,1,0:T(8,128)}, u32[]{:S(2)}) copy-start(f32[8,16,128]{2,1,0:T(8,128)} %param.7) | copy-start | bytes 196612
  0.6 10.3 %copy-start.1 = (s32[2,4,8]{2,1,0:T(4,128)S(1)}, s32[2,4,8]{2,1,0:T(4,128)}, u32[]{:S(2)}) copy-start(s32[2,4,8]{2,1,0:T(4,128)} %param.11) | copy-start | bytes 772
  4.2 7.1 %collective-permute-start = (f32[6,1,16,128]{3,2,1,0:T(8,128)S(1)}, f32[6,1,16,128]{3,2,1,0:T(8,128)S(1)}, u32[]{:S(2)}, u32[]{:S(2)}) collective-permute-start(f32[6,1,16,128]{3,2,1,0:T(8,128)S(1)} %get-tuple-element.37), channel_id=1, source_target_pairs={{0,16},{1,17},{2,18},{3,19},{4,20},{5,21},{6,22},{7,23},{8,24},{9,... | collective-permute-start | bytes 147464 | tf_op jit(solution)/shard_map/ppermute | solution.py:44
  9.1 6.0 %collective-permute-start.1 = (f32[6,1,16,128]{3,2,1,0:T(8,128)S(1)}, f32[6,1,16,128]{3,2,1,0:T(8,128)S(1)}, u32[]{:S(2)}, u32[]{:S(2)}) collective-permute-start(f32[6,1,16,128]{3,2,1,0:T(8,128)S(1)} %get-tuple-element.38), channel_id=1, source_target_pairs={{16,0},{17,1},{18,2},{19,3},{20,4},{21,5},{22,6},{23,7},{24,8},{25... | collective-permute-start | bytes 147464 | tf_op jit(solution)/shard_map/ppermute | solution.py:46
  15.1 5.0 %collective-permute-start.2 = (f32[6,10,1,128]{3,2,1,0:T(1,128)S(1)}, f32[6,10,1,128]{3,2,1,0:T(1,128)S(1)}, u32[]{:S(2)}, u32[]{:S(2)}) collective-permute-start(f32[6,10,1,128]{3,2,1,0:T(1,128)S(1)} %get-tuple-element.35), channel_id=1, source_target_pairs={{0,4},{4,8},{8,12},{1,5},{5,9},{9,13},{2,6},{6,10},{10,14},{3,7},{... | collective-permute-start | bytes 92168 | tf_op jit(solution)/shard_map/ppermute | solution.py:44
  18.6 5.8 %collective-permute-start.3 = (f32[6,10,1,128]{3,2,1,0:T(1,128)S(1)}, f32[6,10,1,128]{3,2,1,0:T(1,128)S(1)}, u32[]{:S(2)}, u32[]{:S(2)}) collective-permute-start(f32[6,10,1,128]{3,2,1,0:T(1,128)S(1)} %get-tuple-element.36), channel_id=1, source_target_pairs={{4,0},{8,4},{12,8},{5,1},{9,5},{13,9},{6,2},{10,6},{14,10},{7,3},{... | collective-permute-start | bytes 92168 | tf_op jit(solution)/shard_map/ppermute | solution.py:46
  25.2 45.1 %collective-permute-start.4 = (f32[6,10,18,1]{2,3,1,0:T(1,128)S(1)}, f32[6,10,18,1]{2,3,1,0:T(1,128)S(1)}, u32[]{:S(2)}, u32[]{:S(2)}) collective-permute-start(f32[6,10,18,1]{2,3,1,0:T(1,128)S(1)} %copy.79), channel_id=1, source_target_pairs={{0,1},{1,2},{2,3},{4,5},{5,6},{6,7},{8,9},{9,10},{10,11},{12,13},{... | collective-permute-start | bytes 12968 | tf_op jit(solution)/shard_map/ppermute | solution.py:44
  27.0 43.8 %collective-permute-start.5 = (f32[6,10,18,1]{2,3,1,0:T(1,128)S(1)}, f32[6,10,18,1]{2,3,1,0:T(1,128)S(1)}, u32[]{:S(2)}, u32[]{:S(2)}) collective-permute-start(f32[6,10,18,1]{2,3,1,0:T(1,128)S(1)} %copy.80), channel_id=1, source_target_pairs={{1,0},{2,1},{3,2},{5,4},{6,5},{7,6},{9,8},{10,9},{11,10},{13,12},{... | collective-permute-start | bytes 12968 | tf_op jit(solution)/shard_map/ppermute | solution.py:46
  140.0 5.9 %collective-permute-start.6 = (f32[1,16,128]{2,1,0:T(8,128)S(1)}, f32[1,16,128]{2,1,0:T(8,128)S(1)}, u32[]{:S(2)}, u32[]{:S(2)}) collective-permute-start(f32[1,16,128]{2,1,0:T(8,128)S(1)} %slice.1082), channel_id=1, source_target_pairs={{16,0},{17,1},{18,2},{19,3},{20,4},{21,5},{22,6},{23,7},{24,8},{25... | collective-permute-start | bytes 24584 | tf_op jit(solution)/shard_map/ppermute | solution.py:46
  141.3 5.9 %collective-permute-start.7 = (f32[1,16,128]{2,1,0:T(8,128)S(1)}, f32[1,16,128]{2,1,0:T(8,128)S(1)}, u32[]{:S(2)}, u32[]{:S(2)}) collective-permute-start(f32[1,16,128]{2,1,0:T(8,128)S(1)} %slice.1082), channel_id=1, source_target_pairs={{0,16},{1,17},{2,18},{3,19},{4,20},{5,21},{6,22},{7,23},{8,24},{9,... | collective-permute-start | bytes 24584 | tf_op jit(solution)/shard_map/ppermute | solution.py:44
  147.2 5.9 %collective-permute-start.8 = (f32[10,1,128]{2,1,0:T(1,128)S(1)}, f32[10,1,128]{2,1,0:T(1,128)S(1)}, u32[]{:S(2)}, u32[]{:S(2)}) collective-permute-start(f32[10,1,128]{2,1,0:T(1,128)S(1)} %get-tuple-element.104), channel_id=1, source_target_pairs={{4,0},{8,4},{12,8},{5,1},{9,5},{13,9},{6,2},{10,6},{14,10},{7,3},{... | collective-permute-start | bytes 15368 | tf_op jit(solution)/shard_map/ppermute | solution.py:46
  148.5 5.9 %collective-permute-start.9 = (f32[10,1,128]{2,1,0:T(1,128)S(1)}, f32[10,1,128]{2,1,0:T(1,128)S(1)}, u32[]{:S(2)}, u32[]{:S(2)}) collective-permute-start(f32[10,1,128]{2,1,0:T(1,128)S(1)} %get-tuple-element.103), channel_id=1, source_target_pairs={{0,4},{4,8},{8,12},{1,5},{5,9},{9,13},{2,6},{6,10},{10,14},{3,7},{... | collective-permute-start | bytes 15368 | tf_op jit(solution)/shard_map/ppermute | solution.py:44
  154.5 4.4 %collective-permute-start.10 = (f32[10,18,1]{2,1,0:T(8,128)S(1)}, f32[10,18,1]{2,1,0:T(8,128)S(1)}, u32[]{:S(2)}, u32[]{:S(2)}) collective-permute-start(f32[10,18,1]{2,1,0:T(8,128)S(1)} %get-tuple-element.68), channel_id=1, source_target_pairs={{1,0},{2,1},{3,2},{5,4},{6,5},{7,6},{9,8},{10,9},{11,10},{13,12},{... | collective-permute-start | bytes 2168 | tf_op jit(solution)/shard_map/ppermute | solution.py:46
  155.8 4.0 collective-permute-start.11
  160.2 5.9 %collective-permute-start.12 = (f32[1,16,128]{2,1,0:T(8,128)S(1)}, f32[1,16,128]{2,1,0:T(8,128)S(1)}, u32[]{:S(2)}, u32[]{:S(2)}) collective-permute-start(f32[1,16,128]{2,1,0:T(8,128)S(1)} %get-tuple-element.110), channel_id=1, source_target_pairs={{16,0},{17,1},{18,2},{19,3},{20,4},{21,5},{22,6},{23,7},{24,8},{25... | collective-permute-start | bytes 24584 | tf_op jit(solution)/shard_map/ppermute | solution.py:46
  161.5 5.9 %collective-permute-start.13 = (f32[1,16,128]{2,1,0:T(8,128)S(1)}, f32[1,16,128]{2,1,0:T(8,128)S(1)}, u32[]{:S(2)}, u32[]{:S(2)}) collective-permute-start(f32[1,16,128]{2,1,0:T(8,128)S(1)} %get-tuple-element.109), channel_id=1, source_target_pairs={{0,16},{1,17},{2,18},{3,19},{4,20},{5,21},{6,22},{7,23},{8,24},{9,... | collective-permute-start | bytes 24584 | tf_op jit(solution)/shard_map/ppermute | solution.py:44
  167.4 6.1 %collective-permute-start.14 = (f32[10,1,128]{2,1,0:T(1,128)S(1)}, f32[10,1,128]{2,1,0:T(1,128)S(1)}, u32[]{:S(2)}, u32[]{:S(2)}) collective-permute-start(f32[10,1,128]{2,1,0:T(1,128)S(1)} %get-tuple-element.100), channel_id=1, source_target_pairs={{4,0},{8,4},{12,8},{5,1},{9,5},{13,9},{6,2},{10,6},{14,10},{7,3},{... | collective-permute-start | bytes 15368 | tf_op jit(solution)/shard_map/ppermute | solution.py:46
  168.7 6.1 %collective-permute-start.15 = (f32[10,1,128]{2,1,0:T(1,128)S(1)}, f32[10,1,128]{2,1,0:T(1,128)S(1)}, u32[]{:S(2)}, u32[]{:S(2)}) collective-permute-start(f32[10,1,128]{2,1,0:T(1,128)S(1)} %get-tuple-element.99), channel_id=1, source_target_pairs={{0,4},{4,8},{8,12},{1,5},{5,9},{9,13},{2,6},{6,10},{10,14},{3,7},{... | collective-permute-start | bytes 15368 | tf_op jit(solution)/shard_map/ppermute | solution.py:44
  175.0 4.6 %collective-permute-start.16 = (f32[10,18,1]{2,1,0:T(8,128)S(1)}, f32[10,18,1]{2,1,0:T(8,128)S(1)}, u32[]{:S(2)}, u32[]{:S(2)}) collective-permute-start(f32[10,18,1]{2,1,0:T(8,128)S(1)} %get-tuple-element.66), channel_id=1, source_target_pairs={{1,0},{2,1},{3,2},{5,4},{6,5},{7,6},{9,8},{10,9},{11,10},{13,12},{... | collective-permute-start | bytes 2168 | tf_op jit(solution)/shard_map/ppermute | solution.py:46
  176.3 4.0 collective-permute-start.17
  230.1 5.8 %collective-permute-start.18 = (f32[1,16,128]{2,1,0:T(8,128)S(1)}, f32[1,16,128]{2,1,0:T(8,128)S(1)}, u32[]{:S(2)}, u32[]{:S(2)}) collective-permute-start(f32[1,16,128]{2,1,0:T(8,128)S(1)} %slice.1129), channel_id=1, source_target_pairs={{16,0},{17,1},{18,2},{19,3},{20,4},{21,5},{22,6},{23,7},{24,8},{25... | collective-permute-start | bytes 24584 | tf_op jit(solution)/shard_map/ppermute | solution.py:46
  231.4 5.9 %collective-permute-start.19 = (f32[1,16,128]{2,1,0:T(8,128)S(1)}, f32[1,16,128]{2,1,0:T(8,128)S(1)}, u32[]{:S(2)}, u32[]{:S(2)}) collective-permute-start(f32[1,16,128]{2,1,0:T(8,128)S(1)} %slice.1129), channel_id=1, source_target_pairs={{0,16},{1,17},{2,18},{3,19},{4,20},{5,21},{6,22},{7,23},{8,24},{9,... | collective-permute-start | bytes 24584 | tf_op jit(solution)/shard_map/ppermute | solution.py:44
  237.3 7.7 %collective-permute-start.20 = (f32[10,1,128]{2,1,0:T(1,128)S(1)}, f32[10,1,128]{2,1,0:T(1,128)S(1)}, u32[]{:S(2)}, u32[]{:S(2)}) collective-permute-start(f32[10,1,128]{2,1,0:T(1,128)S(1)} %get-tuple-element.96), channel_id=1, source_target_pairs={{4,0},{8,4},{12,8},{5,1},{9,5},{13,9},{6,2},{10,6},{14,10},{7,3},{... | collective-permute-start | bytes 15368 | tf_op jit(solution)/shard_map/ppermute | solution.py:46
  238.6 6.4 %collective-permute-start.21 = (f32[10,1,128]{2,1,0:T(1,128)S(1)}, f32[10,1,128]{2,1,0:T(1,128)S(1)}, u32[]{:S(2)}, u32[]{:S(2)}) collective-permute-start(f32[10,1,128]{2,1,0:T(1,128)S(1)} %get-tuple-element.95), channel_id=1, source_target_pairs={{0,4},{4,8},{8,12},{1,5},{5,9},{9,13},{2,6},{6,10},{10,14},{3,7},{... | collective-permute-start | bytes 15368 | tf_op jit(solution)/shard_map/ppermute | solution.py:44
  245.2 4.4 %collective-permute-start.22 = (f32[10,18,1]{2,1,0:T(8,128)S(1)}, f32[10,18,1]{2,1,0:T(8,128)S(1)}, u32[]{:S(2)}, u32[]{:S(2)}) collective-permute-start(f32[10,18,1]{2,1,0:T(8,128)S(1)} %get-tuple-element.64), channel_id=1, source_target_pairs={{1,0},{2,1},{3,2},{5,4},{6,5},{7,6},{9,8},{10,9},{11,10},{13,12},{... | collective-permute-start | bytes 2168 | tf_op jit(solution)/shard_map/ppermute | solution.py:46
  246.5 4.0 collective-permute-start.23
  250.9 5.9 %collective-permute-start.24 = (f32[1,16,128]{2,1,0:T(8,128)S(1)}, f32[1,16,128]{2,1,0:T(8,128)S(1)}, u32[]{:S(2)}, u32[]{:S(2)}) collective-permute-start(f32[1,16,128]{2,1,0:T(8,128)S(1)} %get-tuple-element.108), channel_id=1, source_target_pairs={{16,0},{17,1},{18,2},{19,3},{20,4},{21,5},{22,6},{23,7},{24,8},{25... | collective-permute-start | bytes 24584 | tf_op jit(solution)/shard_map/ppermute | solution.py:46
  252.2 5.9 %collective-permute-start.25 = (f32[1,16,128]{2,1,0:T(8,128)S(1)}, f32[1,16,128]{2,1,0:T(8,128)S(1)}, u32[]{:S(2)}, u32[]{:S(2)}) collective-permute-start(f32[1,16,128]{2,1,0:T(8,128)S(1)} %get-tuple-element.107), channel_id=1, source_target_pairs={{0,16},{1,17},{2,18},{3,19},{4,20},{5,21},{6,22},{7,23},{8,24},{9,... | collective-permute-start | bytes 24584 | tf_op jit(solution)/shard_map/ppermute | solution.py:44
  258.1 5.9 %collective-permute-start.26 = (f32[10,1,128]{2,1,0:T(1,128)S(1)}, f32[10,1,128]{2,1,0:T(1,128)S(1)}, u32[]{:S(2)}, u32[]{:S(2)}) collective-permute-start(f32[10,1,128]{2,1,0:T(1,128)S(1)} %get-tuple-element.92), channel_id=1, source_target_pairs={{4,0},{8,4},{12,8},{5,1},{9,5},{13,9},{6,2},{10,6},{14,10},{7,3},{... | collective-permute-start | bytes 15368 | tf_op jit(solution)/shard_map/ppermute | solution.py:46
  259.4 5.9 %collective-permute-start.27 = (f32[10,1,128]{2,1,0:T(1,128)S(1)}, f32[10,1,128]{2,1,0:T(1,128)S(1)}, u32[]{:S(2)}, u32[]{:S(2)}) collective-permute-start(f32[10,1,128]{2,1,0:T(1,128)S(1)} %get-tuple-element.91), channel_id=1, source_target_pairs={{0,4},{4,8},{8,12},{1,5},{5,9},{9,13},{2,6},{6,10},{10,14},{3,7},{... | collective-permute-start | bytes 15368 | tf_op jit(solution)/shard_map/ppermute | solution.py:44
  265.4 4.6 %collective-permute-start.28 = (f32[10,18,1]{2,1,0:T(8,128)S(1)}, f32[10,18,1]{2,1,0:T(8,128)S(1)}, u32[]{:S(2)}, u32[]{:S(2)}) collective-permute-start(f32[10,18,1]{2,1,0:T(8,128)S(1)} %get-tuple-element.62), channel_id=1, source_target_pairs={{1,0},{2,1},{3,2},{5,4},{6,5},{7,6},{9,8},{10,9},{11,10},{13,12},{... | collective-permute-start | bytes 2168 | tf_op jit(solution)/shard_map/ppermute | solution.py:46
  266.7 4.2 %collective-permute-start.29 = (f32[10,18,1]{2,1,0:T(8,128)S(1)}, f32[10,18,1]{2,1,0:T(8,128)S(1)}, u32[]{:S(2)}, u32[]{:S(2)}) collective-permute-start(f32[10,18,1]{2,1,0:T(8,128)S(1)} %get-tuple-element.61), channel_id=1, source_target_pairs={{0,1},{1,2},{2,3},{4,5},{5,6},{6,7},{8,9},{9,10},{10,11},{12,13},{... | collective-permute-start | bytes 2168 | tf_op jit(solution)/shard_map/ppermute | solution.py:44
  322.5 16.1 %collective-permute-start.36 = (f32[1,16,128]{2,1,0:T(8,128)S(1)}, f32[1,16,128]{2,1,0:T(8,128)S(1)}, u32[]{:S(2)}, u32[]{:S(2)}) collective-permute-start(f32[1,16,128]{2,1,0:T(8,128)S(1)} %slice.1200), channel_id=1, source_target_pairs={{16,0},{17,1},{18,2},{19,3},{20,4},{21,5},{22,6},{23,7},{24,8},{25... | collective-permute-start | bytes 24584 | tf_op jit(solution)/shard_map/ppermute | solution.py:46
  323.8 14.8 %collective-permute-start.37 = (f32[1,16,128]{2,1,0:T(8,128)S(1)}, f32[1,16,128]{2,1,0:T(8,128)S(1)}, u32[]{:S(2)}, u32[]{:S(2)}) collective-permute-start(f32[1,16,128]{2,1,0:T(8,128)S(1)} %slice.1200), channel_id=1, source_target_pairs={{0,16},{1,17},{2,18},{3,19},{4,20},{5,21},{6,22},{7,23},{8,24},{9,... | collective-permute-start | bytes 24584 | tf_op jit(solution)/shard_map/ppermute | solution.py:44
  332.8 11.8 %collective-permute-start.30 = (f32[1,16,128]{2,1,0:T(8,128)S(1)}, f32[1,16,128]{2,1,0:T(8,128)S(1)}, u32[]{:S(2)}, u32[]{:S(2)}) collective-permute-start(f32[1,16,128]{2,1,0:T(8,128)S(1)} %get-tuple-element.106), channel_id=1, source_target_pairs={{16,0},{17,1},{18,2},{19,3},{20,4},{21,5},{22,6},{23,7},{24,8},{25... | collective-permute-start | bytes 24584 | tf_op jit(solution)/shard_map/ppermute | solution.py:46
  334.1 10.5 %collective-permute-start.31 = (f32[1,16,128]{2,1,0:T(8,128)S(1)}, f32[1,16,128]{2,1,0:T(8,128)S(1)}, u32[]{:S(2)}, u32[]{:S(2)}) collective-permute-start(f32[1,16,128]{2,1,0:T(8,128)S(1)} %get-tuple-element.105), channel_id=1, source_target_pairs={{0,16},{1,17},{2,18},{3,19},{4,20},{5,21},{6,22},{7,23},{8,24},{9,... | collective-permute-start | bytes 24584 | tf_op jit(solution)/shard_map/ppermute | solution.py:44
  338.7 11.8 %collective-permute-start.38 = (f32[10,1,128]{2,1,0:T(1,128)S(1)}, f32[10,1,128]{2,1,0:T(1,128)S(1)}, u32[]{:S(2)}, u32[]{:S(2)}) collective-permute-start(f32[10,1,128]{2,1,0:T(1,128)S(1)} %get-tuple-element.84), channel_id=1, source_target_pairs={{4,0},{8,4},{12,8},{5,1},{9,5},{13,9},{6,2},{10,6},{14,10},{7,3},{... | collective-permute-start | bytes 15368 | tf_op jit(solution)/shard_map/ppermute | solution.py:46
  340.0 10.5 %collective-permute-start.39 = (f32[10,1,128]{2,1,0:T(1,128)S(1)}, f32[10,1,128]{2,1,0:T(1,128)S(1)}, u32[]{:S(2)}, u32[]{:S(2)}) collective-permute-start(f32[10,1,128]{2,1,0:T(1,128)S(1)} %get-tuple-element.83), channel_id=1, source_target_pairs={{0,4},{4,8},{8,12},{1,5},{5,9},{9,13},{2,6},{6,10},{10,14},{3,7},{... | collective-permute-start | bytes 15368 | tf_op jit(solution)/shard_map/ppermute | solution.py:44
  344.6 10.3 %collective-permute-start.32 = (f32[10,1,128]{2,1,0:T(1,128)S(1)}, f32[10,1,128]{2,1,0:T(1,128)S(1)}, u32[]{:S(2)}, u32[]{:S(2)}) collective-permute-start(f32[10,1,128]{2,1,0:T(1,128)S(1)} %get-tuple-element.88), channel_id=1, source_target_pairs={{4,0},{8,4},{12,8},{5,1},{9,5},{13,9},{6,2},{10,6},{14,10},{7,3},{... | collective-permute-start | bytes 15368 | tf_op jit(solution)/shard_map/ppermute | solution.py:46
  345.9 9.1 %collective-permute-start.33 = (f32[10,1,128]{2,1,0:T(1,128)S(1)}, f32[10,1,128]{2,1,0:T(1,128)S(1)}, u32[]{:S(2)}, u32[]{:S(2)}) collective-permute-start(f32[10,1,128]{2,1,0:T(1,128)S(1)} %get-tuple-element.87), channel_id=1, source_target_pairs={{0,4},{4,8},{8,12},{1,5},{5,9},{9,13},{2,6},{6,10},{10,14},{3,7},{... | collective-permute-start | bytes 15368 | tf_op jit(solution)/shard_map/ppermute | solution.py:44
  350.6 54.2 %collective-permute-start.40 = (f32[10,18,1]{2,1,0:T(8,128)S(1)}, f32[10,18,1]{2,1,0:T(8,128)S(1)}, u32[]{:S(2)}, u32[]{:S(2)}) collective-permute-start(f32[10,18,1]{2,1,0:T(8,128)S(1)} %get-tuple-element.58), channel_id=1, source_target_pairs={{1,0},{2,1},{3,2},{5,4},{6,5},{7,6},{9,8},{10,9},{11,10},{13,12},{... | collective-permute-start | bytes 2168 | tf_op jit(solution)/shard_map/ppermute | solution.py:46
  351.9 52.9 %collective-permute-start.41 = (f32[10,18,1]{2,1,0:T(8,128)S(1)}, f32[10,18,1]{2,1,0:T(8,128)S(1)}, u32[]{:S(2)}, u32[]{:S(2)}) collective-permute-start(f32[10,18,1]{2,1,0:T(8,128)S(1)} %get-tuple-element.57), channel_id=1, source_target_pairs={{0,1},{1,2},{2,3},{4,5},{5,6},{6,7},{8,9},{9,10},{10,11},{12,13},{... | collective-permute-start | bytes 2168 | tf_op jit(solution)/shard_map/ppermute | solution.py:44
  355.1 6.0 %collective-permute-start.34 = (f32[10,18,1]{2,1,0:T(8,128)S(1)}, f32[10,18,1]{2,1,0:T(8,128)S(1)}, u32[]{:S(2)}, u32[]{:S(2)}) collective-permute-start(f32[10,18,1]{2,1,0:T(8,128)S(1)} %get-tuple-element.60), channel_id=1, source_target_pairs={{1,0},{2,1},{3,2},{5,4},{6,5},{7,6},{9,8},{10,9},{11,10},{13,12},{... | collective-permute-start | bytes 2168 | tf_op jit(solution)/shard_map/ppermute | solution.py:46
  356.4 5.6 %collective-permute-start.35 = (f32[10,18,1]{2,1,0:T(8,128)S(1)}, f32[10,18,1]{2,1,0:T(8,128)S(1)}, u32[]{:S(2)}, u32[]{:S(2)}) collective-permute-start(f32[10,18,1]{2,1,0:T(8,128)S(1)} %get-tuple-element.59), channel_id=1, source_target_pairs={{0,1},{1,2},{2,3},{4,5},{5,6},{6,7},{8,9},{9,10},{10,11},{12,13},{... | collective-permute-start | bytes 2168 | tf_op jit(solution)/shard_map/ppermute | solution.py:44
